TPU v7x, 32 devices: a whole 2x2x4 slice. The times are simulated.
32 devices in a mesh: geo: 4 (over x, core), comp: 8 (over z, y).
Axes of the slice: x: 2, y: 2, z: 4, core: 2. Of those that a mesh axis runs over, the one named last changes fastest.
Arguments:
- spectrum: bfloat16 [1152, 512, 128], P('comp', 'geo'), may hold values from 0.049804688 to 1
- land_mask: int32 [512, 128], P('geo'), may hold values 0 or 1
- wind_speed: float32 [512, 128], P('geo'), may hold values from 0.5 to 2
- wind_dir: float32 [512, 128], P('geo'), may hold values from -3.140625 to 3.140625
- input_rate: float32 [1152], P('comp'), may hold values from 0.05 to 0.5
- dissipation: float32 [1152], replicated, may hold values from 0.05 to 0.5
- pair_first: bfloat16 [1728, 1152], replicated, may hold values from -0.1875 to 0.1875
- pair_second: bfloat16 [1728, 1152], replicated, may hold values from -0.1875 to 0.1875
- merge_weight: bfloat16 [1152, 1728], replicated, may hold values from -0.15625 to 0.15625
Outputs:
- spectrum_next: bfloat16 [1152, 512, 128], P('comp', 'geo')
All inputs are finite; a program needn't handle non-finite values. No bound on the sum of `land_mask` on one device may be relied on, other than what follows from the above.
Results may differ from a plain program's by a relative error of at most 0.0038.
Values may be sent and summed in bfloat16 or wider, within the bound.
A program may use at most 128 MiB of HBM per device.

v0:
```python
import math

import jax
import jax.numpy as jnp
from jax import lax
from jax.sharding import PartitionSpec as P

ND = 36
M = 1152
PROP_STEPS = 6


def with_halo(cells, sides, width):
    for axis, dim in sides:
        count = lax.axis_size(axis)
        ends = count - 1
        head = lax.slice_in_dim(cells, 0, width, axis=dim)
        tail = lax.slice_in_dim(cells, cells.shape[dim] - width, cells.shape[dim], axis=dim)
        cells = jnp.concatenate(
            [
                lax.ppermute(tail, axis, [(i, (i + 1) % count) for i in range(ends)]),
                cells,
                lax.ppermute(head, axis, [((i + 1) % count, i) for i in range(ends)]),
            ],
            axis=dim,
        )
    return cells


def upwind(padded, sea_mask, speed_x, speed_y):
    center = padded[:, 1:-1]
    lower = padded[:, :-2]
    upper = padded[:, 2:]
    western = jnp.roll(center, 1, axis=2)
    eastern = jnp.roll(center, -1, axis=2)
    change = jnp.maximum(speed_x, 0.0) * (center - western) + jnp.maximum(-speed_x, 0.0) * (
        center - eastern
    )
    change = (
        change
        + jnp.maximum(speed_y, 0.0) * (center - lower)
        + jnp.maximum(-speed_y, 0.0) * (center - upper)
    )
    return (center - change) * sea_mask


def point_terms(points, dissipation, pair_first, pair_second, merge_weight):
    count_comps, count_rows, count_cols = points.shape
    spectra = points.reshape(count_comps, count_rows * count_cols)
    first_proj = jnp.dot(pair_first, spectra, preferred_element_type=jnp.float32)
    second_proj = jnp.dot(pair_second, spectra, preferred_element_type=jnp.float32)
    product = (first_proj * second_proj).astype(jnp.bfloat16)
    transfer = jnp.dot(merge_weight, product, preferred_element_type=jnp.float32)
    energy = jnp.sum(spectra, axis=0, dtype=jnp.float32)
    whitecap = (
        -dissipation[:, None] * jnp.sqrt(energy / M + 1e-06)[None, :] * spectra.astype(jnp.float32)
    )
    increment = (transfer + whitecap).astype(jnp.bfloat16)
    return increment.reshape(count_comps, count_rows, count_cols)


def body(
    spectrum,
    land_mask,
    wind_speed,
    wind_dir,
    input_rate,
    dissipation,
    pair_first,
    pair_second,
    merge_weight,
):
    local_comps = spectrum.shape[0]
    comp_ids = lax.axis_index("comp") * local_comps + jnp.arange(local_comps, dtype=jnp.int32)
    frequency = (comp_ids // ND).astype(jnp.float32)
    heading = 2.0 * math.pi * (comp_ids % ND).astype(jnp.float32) / ND
    courant = 0.7 * jnp.power(jnp.float32(1.1), -frequency)
    speed_x = (courant * jnp.cos(heading))[:, None, None]
    speed_y = (courant * jnp.sin(heading))[:, None, None]
    sea_mask = land_mask.astype(jnp.float32)
    density = spectrum.astype(jnp.float32)

    def advance(current):
        padded = with_halo(current, (("geo", 1),), 1)
        return upwind(padded, sea_mask, speed_x, speed_y)

    for substep in range(PROP_STEPS):
        density = advance(density)
    outgoing = density.astype(jnp.bfloat16)
    gathered = lax.all_to_all(outgoing, "comp", split_axis=1, concat_axis=0, tiled=True)
    returned = lax.all_to_all(
        point_terms(gathered, dissipation, pair_first, pair_second, merge_weight),
        "comp",
        split_axis=0,
        concat_axis=1,
        tiled=True,
    )
    facing = jnp.maximum(jnp.cos(heading[:, None, None] - wind_dir[None]), 0.0)
    growth = input_rate[:, None, None] * wind_speed[None] * facing * facing
    density = density + growth * density + returned.astype(jnp.float32)
    density = advance(density)
    return density.astype(jnp.bfloat16)


def solution(mesh):
    placed = (
        P("comp", "geo", None),
        P("geo", None),
        P("geo", None),
        P("geo", None),
        P("comp"),
        P(),
        P(),
        P(),
        P(),
    )
    return jax.shard_map(
        body, mesh=mesh, in_specs=placed, out_specs=P("comp", "geo", None), check_vma=False
    )
```

profile of v0, /device:TPU:1, one launch (start us, length us, event | category | flops | bytes accessed | tf_op | source)
XLA Modules:
  0.0 674.7 jit_solution(10085069956192810546)
XLA Ops:
  7.6 12.0 %fusion.102 = (f32[144,128,127]{2,1,0:T(8,128)}, f32[144,128,127]{2,1,0:T(8,128)}) fusion(bf16[144,128,128]{2,1,0:T(8,128)(2,1)} %param.9), kind=kLoop, calls=%fused_computation.150 | loop fusion | bytes 37453824 | tf_op jit(solution)/shard_map/jit(_roll_static)/slice | solution.py:35
  19.6 12.1 %fusion.103 = (f32[144,128,1]{2,1,0:T(8,128)}, f32[144,128,1]{2,1,0:T(8,128)}) fusion(bf16[144,128,128]{2,1,0:T(8,128)(2,1)} %param.9), kind=kLoop, calls=%fused_computation.151 | loop fusion | bytes 294912 | tf_op jit(solution)/shard_map/jit(_roll_static)/slice | solution.py:35
  31.7 7.3 %convert_element_type.73 = f32[144,128,128]{2,1,0:T(8,128)} convert(bf16[144,128,128]{2,1,0:T(8,128)(2,1)} %param.9) | non-fusion elementwise | flops 2359296 | bytes 14155776 | tf_op jit(solution)/shard_map/convert_element_type | solution.py:81
  39.1 23.7 %fusion.7 = f32[144,128,128]{2,1,0:T(8,128)S(1)} fusion(bf16[144,128,128]{2,1,0:T(8,128)(2,1)} %param.9, f32[144,1,128]{2,1,0:T(1,128)S(1)} %collective-permute-done.1, f32[144,128,128]{2,1,0:T(8,128)} %convert_element_type.73, f32[144,1,128]{2,1,0:T(1,128)S(1)} %collective-permute-done, f32[144,128,127]{2,1,0:T(8,128)} %get-tuple-element.44, ...), kind=kLoop, calls=%fused_computation.15 | loop fusion | flops 42467328 | bytes 42682624 | tf_op jit(solution)/shard_map/mul | solution.py:44
  62.8 8.6 %fusion.99 = (f32[144,128,127]{2,1,0:T(8,128)}, f32[144,128,127]{2,1,0:T(8,128)}) fusion(f32[144,128,128]{2,1,0:T(8,128)S(1)} %fusion.7), kind=kLoop, calls=%fused_computation.147 | loop fusion | bytes 37453824 | tf_op jit(solution)/shard_map/jit(_roll_static)/slice | solution.py:35
  77.3 8.2 %fusion.100 = (f32[144,128,1]{2,1,0:T(8,128)}, f32[144,128,1]{2,1,0:T(8,128)}) fusion(f32[144,128,128]{2,1,0:T(8,128)S(1)} %fusion.7), kind=kLoop, calls=%fused_computation.148 | loop fusion | bytes 294912 | tf_op jit(solution)/shard_map/jit(_roll_static)/slice | solution.py:35
  85.6 26.0 %fusion.54 = f32[144,128,128]{2,1,0:T(8,128)S(1)} fusion(f32[144,128,128]{2,1,0:T(8,128)} %copy-done.3, f32[144,1,128]{2,1,0:T(1,128)S(1)} %collective-permute-done.3, f32[144,1,128]{2,1,0:T(1,128)S(1)} %collective-permute-done.2, f32[144,128,127]{2,1,0:T(8,128)} %get-tuple-element.38, f32[144,128,1]{2,1,0:T(8,128)} %get-tuple-element.40, ...), kind=kLoop, calls=%fused_computation.73 | loop fusion | flops 40108032 | bytes 37964032 | tf_op jit(solution)/shard_map/mul | solution.py:44
  111.6 8.1 %fusion.96 = (f32[144,128,127]{2,1,0:T(8,128)}, f32[144,128,127]{2,1,0:T(8,128)}) fusion(f32[144,128,128]{2,1,0:T(8,128)S(1)} %fusion.54), kind=kLoop, calls=%fused_computation.144 | loop fusion | bytes 37453824 | tf_op jit(solution)/shard_map/jit(_roll_static)/slice | solution.py:35
  125.7 8.2 %fusion.97 = (f32[144,128,1]{2,1,0:T(8,128)}, f32[144,128,1]{2,1,0:T(8,128)}) fusion(f32[144,128,128]{2,1,0:T(8,128)S(1)} %fusion.54), kind=kLoop, calls=%fused_computation.145 | loop fusion | bytes 294912 | tf_op jit(solution)/shard_map/jit(_roll_static)/slice | solution.py:35
  133.9 19.3 %fusion.46 = f32[144,128,128]{2,1,0:T(8,128)} fusion(f32[144,128,128]{2,1,0:T(8,128)S(1)} %fusion.54, f32[144,1,128]{2,1,0:T(1,128)S(1)} %collective-permute-done.5, f32[144,1,128]{2,1,0:T(1,128)S(1)} %collective-permute-done.4, f32[144,128,127]{2,1,0:T(8,128)} %get-tuple-element.32, f32[144,128,1]{2,1,0:T(8,128)} %get-tuple-element.34, ...), kind=kLoop, calls=%fused_computation.63 | loop fusion | flops 40108032 | bytes 37964032 | tf_op jit(solution)/shard_map/mul | solution.py:44
  153.3 14.7 %fusion.93 = (f32[144,128,127]{2,1,0:T(8,128)}, f32[144,128,127]{2,1,0:T(8,128)}) fusion(f32[144,128,128]{2,1,0:T(8,128)} %fusion.46), kind=kLoop, calls=%fused_computation.141 | loop fusion | bytes 37453824 | tf_op jit(solution)/shard_map/jit(_roll_static)/slice | solution.py:35
  173.9 8.2 %fusion.94 = (f32[144,128,1]{2,1,0:T(8,128)}, f32[144,128,1]{2,1,0:T(8,128)}) fusion(f32[144,128,128]{2,1,0:T(8,128)S(1)} %copy-done), kind=kLoop, calls=%fused_computation.142 | loop fusion | bytes 294912 | tf_op jit(solution)/shard_map/jit(_roll_static)/slice | solution.py:35
  182.2 19.3 %fusion.38 = f32[144,128,128]{2,1,0:T(8,128)} fusion(f32[144,128,128]{2,1,0:T(8,128)S(1)} %copy-done, f32[144,1,128]{2,1,0:T(1,128)S(1)} %collective-permute-done.7, f32[144,1,128]{2,1,0:T(1,128)S(1)} %collective-permute-done.6, f32[144,128,127]{2,1,0:T(8,128)} %get-tuple-element.26, f32[144,128,1]{2,1,0:T(8,128)} %get-tuple-element.28, ...), kind=kLoop, calls=%fused_computation.53 | loop fusion | flops 40108032 | bytes 37964032 | tf_op jit(solution)/shard_map/mul | solution.py:44
  201.5 14.7 %fusion.90 = (f32[144,128,127]{2,1,0:T(8,128)}, f32[144,128,127]{2,1,0:T(8,128)}) fusion(f32[144,128,128]{2,1,0:T(8,128)} %fusion.38), kind=kLoop, calls=%fused_computation.138 | loop fusion | bytes 37453824 | tf_op jit(solution)/shard_map/jit(_roll_static)/slice | solution.py:35
  222.4 8.2 %fusion.91 = (f32[144,128,1]{2,1,0:T(8,128)}, f32[144,128,1]{2,1,0:T(8,128)}) fusion(f32[144,128,128]{2,1,0:T(8,128)S(1)} %copy-done.1), kind=kLoop, calls=%fused_computation.139 | loop fusion | bytes 294912 | tf_op jit(solution)/shard_map/jit(_roll_static)/slice | solution.py:35
  230.6 19.3 %fusion.30 = f32[144,128,128]{2,1,0:T(8,128)} fusion(f32[144,128,128]{2,1,0:T(8,128)S(1)} %copy-done.1, f32[144,1,128]{2,1,0:T(1,128)S(1)} %collective-permute-done.9, f32[144,1,128]{2,1,0:T(1,128)S(1)} %collective-permute-done.8, f32[144,128,127]{2,1,0:T(8,128)} %get-tuple-element.20, f32[144,128,1]{2,1,0:T(8,128)} %get-tuple-element.22, ...), kind=kLoop, calls=%fused_computation.43 | loop fusion | flops 40108032 | bytes 37964032 | tf_op jit(solution)/shard_map/mul | solution.py:44
  250.0 14.7 %fusion.87 = (f32[144,128,1]{2,1,0:T(8,128)}, f32[144,128,1]{2,1,0:T(8,128)}) fusion(f32[144,128,128]{2,1,0:T(8,128)} %fusion.30), kind=kLoop, calls=%fused_computation.135 | loop fusion | bytes 294912 | tf_op jit(solution)/shard_map/jit(_roll_static)/slice | solution.py:34
  270.5 8.2 %fusion.88 = (f32[144,128,127]{2,1,0:T(8,128)}, f32[144,128,127]{2,1,0:T(8,128)}) fusion(f32[144,128,128]{2,1,0:T(8,128)S(1)} %copy-done.2), kind=kLoop, calls=%fused_computation.136 | loop fusion | bytes 37453824 | tf_op jit(solution)/shard_map/jit(_roll_static)/slice | solution.py:34
  278.7 19.2 %fusion.82 = (bf16[144,128,128]{2,1,0:T(8,128)(2,1)S(1)}, f32[144,128,128]{2,1,0:T(8,128)}) fusion(f32[128,128]{1,0:T(8,128)S(1)} %convert_element_type.76, f32[144,128,128]{2,1,0:T(8,128)S(1)} %copy-done.2, f32[144,1,128]{2,1,0:T(1,128)S(1)} %collective-permute-done.11, f32[144]{0:T(256)S(1)} %get-tuple-element.49, ...), kind=kLoop, calls=%fused_computation.131 | loop fusion | flops 42467328 | bytes 42682624 | tf_op jit(solution)/shard_map/convert_element_type | solution.py:89
  297.9 5.2 copy.19
  303.2 5.8 all-to-all-start
  309.0 104.0 %all-to-all-done = bf16[144,128,128]{2,0,1:T(8,128)(2,1)} async-done(((bf16[144,128,128]{2,0,1:T(8,128)(2,1)}), bf16[144,128,128]{2,0,1:T(8,128)(2,1)}, u32[]{:S(2)}, u32[]{:S(2)}) %all-to-all-start) | async-done | bytes 4718624 | tf_op jit(solution)/shard_map/all_to_all | solution.py:90
  416.6 5.3 convert_reduce_fusion
  426.5 11.8 %fusion.81 = f32[2048,1728]{0,1:T(8,128)} fusion(bf16[1728,1152]{1,0:T(8,128)(2,1)S(1)} %copy-done.10, bf16[144,8,16,128]{3,2,1,0:T(8,128)(2,1)S(1)} %bitcast.28), kind=kOutput, calls=%fused_computation.130 | convolution fusion | flops 8153726976 | bytes 22855680 | tf_op jit(solution)/shard_map/dot_general | solution.py:50
  438.3 6.8 %copy.21 = bf16[1152,2048]{0,1:T(8,128)(2,1)} copy(bf16[1152,2048]{1,0:T(8,128)(2,1)} %bitcast.30) | data formatting | bytes 9437184 | tf_op jit(solution)/shard_map/reshape | solution.py:49
  445.1 29.8 %fusion.76 = bf16[1152,2048]{0,1:T(8,128)(2,1)} fusion(bf16[1152,2048]{0,1:T(8,128)(2,1)} %copy.21, bf16[1152,1728]{0,1:T(8,128)(2,1)} %param.17, f32[2048,1728]{0,1:T(8,128)} %fusion.81, bf16[1728,1152]{1,0:T(8,128)(2,1)} %param.16, f32[2048]{0:T(1024)S(1)} %sqrt_bitcast_fusion, f32[1152]{0:T(1024)S(1)} %neg.51, bf16[144,8,16,128]{3,2,1,0:T(8,128)(2,1)} %bitcast.29), kind=kOutput, calls=%fused_computation.112 | convolution fusion | flops 16326328320 | bytes 36286976 | tf_op jit(solution)/shard_map/dot_general | solution.py:53
  474.9 7.1 %copy.22 = bf16[1152,16,128]{2,1,0:T(8,128)(2,1)} copy(bf16[1152,16,128]{0,2,1:T(8,128)(2,1)} %bitcast.31) | data formatting | bytes 9437184 | tf_op jit(solution)/shard_map/reshape | solution.py:59
  486.9 105.1 %all-to-all-done.1 = bf16[1152,16,128]{2,1,0:T(8,128)(2,1)} async-done(((bf16[1152,16,128]{2,1,0:T(8,128)(2,1)}), bf16[1152,16,128]{2,1,0:T(8,128)(2,1)}, u32[]{:S(2)}, u32[]{:S(2)}) %all-to-all-start.1) | async-done | bytes 4718624 | tf_op jit(solution)/shard_map/all_to_all | solution.py:91
  600.4 34.9 %fusion.8 = f32[144,128,128]{2,1,0:T(8,128)S(1)} fusion(f32[144,128,128]{2,1,0:T(8,128)} %get-tuple-element.6, f32[144,8,16,128]{3,2,1,0:T(8,128)} %copy.23, f32[128,128]{1,0:T(8,128)S(1)} %copy-done.5, f32[144]{0:T(256)S(1)} %fusion.78, f32[128,128]{1,0:T(8,128)S(1)} %copy-done.6, f32[144]{0:T(256)S(1)} %copy-done.9), kind=kLoop, calls=%fused_computation.16 | loop fusion | flops 18874368 | bytes 28443776 | tf_op jit(solution)/shard_map/add | solution.py:100
  635.3 8.3 %fusion.85 = (f32[144,128,1]{2,1,0:T(8,128)}, f32[144,128,1]{2,1,0:T(8,128)}) fusion(f32[144,128,128]{2,1,0:T(8,128)S(1)} %fusion.8), kind=kLoop, calls=%fused_computation.133 | loop fusion | bytes 294912 | tf_op jit(solution)/shard_map/jit(_roll_static)/slice | solution.py:35
  648.1 8.1 %fusion.84 = (f32[144,128,127]{2,1,0:T(8,128)}, f32[144,128,127]{2,1,0:T(8,128)}) fusion(f32[144,128,128]{2,1,0:T(8,128)S(1)} %fusion.8), kind=kLoop, calls=%fused_computation.132 | loop fusion | bytes 37453824 | tf_op jit(solution)/shard_map/jit(_roll_static)/slice | solution.py:35
  656.2 18.0 %fusion.14 = bf16[144,128,128]{2,1,0:T(8,128)(2,1)} fusion(f32[144,128,128]{2,1,0:T(8,128)S(1)} %fusion.8, f32[144,1,128]{2,1,0:T(1,128)S(1)} %collective-permute-done.13, f32[144,1,128]{2,1,0:T(1,128)S(1)} %collective-permute-done.12, f32[144,128,127]{2,1,0:T(8,128)} %get-tuple-element.8, f32[144,128,1]{2,1,0:T(8,128)} %get-tuple-element.10, ...), kind=kLoop, calls=%fused_computation.23 | loop fusion | flops 42467328 | bytes 33245440 | tf_op jit(solution)/shard_map/convert_element_type | solution.py:102
  (68 shorter events, 63.4 us)
Async XLA Ops:
  1.2 38.0 %collective-permute-start = (f32[144,1,128]{2,1,0:T(1,128)S(1)}, f32[144,1,128]{2,1,0:T(1,128)S(1)}, u32[]{:S(2)}, u32[]{:S(2)}) collective-permute-start(f32[144,1,128]{2,1,0:T(1,128)S(1)} %get-tuple-element.47), channel_id=1, source_target_pairs={{0,8},{8,16},{16,24},{1,9},{9,17},{17,25},{2,10},{10,18},{18,26},{... | collective-permute-start | bytes 221192 | tf_op jit(solution)/shard_map/ppermute | solution.py:21
  5.7 33.5 %collective-permute-start.1 = (f32[144,1,128]{2,1,0:T(1,128)S(1)}, f32[144,1,128]{2,1,0:T(1,128)S(1)}, u32[]{:S(2)}, u32[]{:S(2)}) collective-permute-start(f32[144,1,128]{2,1,0:T(1,128)S(1)} %get-tuple-element.48), channel_id=1, source_target_pairs={{8,0},{16,8},{24,16},{9,1},{17,9},{25,17},{10,2},{18,10},{26,18},{... | collective-permute-start | bytes 221192 | tf_op jit(solution)/shard_map/ppermute | solution.py:23
  31.7 7.3 %copy-start.7 = (s32[128,128]{1,0:T(8,128)S(1)}, s32[128,128]{1,0:T(8,128)}, u32[]{:S(2)}) copy-start(s32[128,128]{1,0:T(8,128)} %param.10) | copy-start | bytes 196612
  62.8 14.5 %copy-start.3 = (f32[144,128,128]{2,1,0:T(8,128)}, f32[144,128,128]{2,1,0:T(8,128)S(1)}, u32[]{:S(2)}) copy-start(f32[144,128,128]{2,1,0:T(8,128)S(1)} %fusion.7) | copy-start | bytes 28311556
  71.5 14.0 %collective-permute-start.2 = (f32[144,1,128]{2,1,0:T(1,128)S(1)}, f32[144,1,128]{2,1,0:T(1,128)S(1)}, u32[]{:S(2)}, u32[]{:S(2)}) collective-permute-start(f32[144,1,128]{2,1,0:T(1,128)S(1)} %get-tuple-element.41), channel_id=1, source_target_pairs={{0,8},{8,16},{16,24},{1,9},{9,17},{17,25},{2,10},{10,18},{18,26},{... | collective-permute-start | bytes 221192 | tf_op jit(solution)/shard_map/ppermute | solution.py:21
  75.2 10.4 %collective-permute-start.3 = (f32[144,1,128]{2,1,0:T(1,128)S(1)}, f32[144,1,128]{2,1,0:T(1,128)S(1)}, u32[]{:S(2)}, u32[]{:S(2)}) collective-permute-start(f32[144,1,128]{2,1,0:T(1,128)S(1)} %get-tuple-element.42), channel_id=1, source_target_pairs={{8,0},{16,8},{24,16},{9,1},{17,9},{25,17},{10,2},{18,10},{26,18},{... | collective-permute-start | bytes 221192 | tf_op jit(solution)/shard_map/ppermute | solution.py:23
  119.8 14.1 %collective-permute-start.4 = (f32[144,1,128]{2,1,0:T(1,128)S(1)}, f32[144,1,128]{2,1,0:T(1,128)S(1)}, u32[]{:S(2)}, u32[]{:S(2)}) collective-permute-start(f32[144,1,128]{2,1,0:T(1,128)S(1)} %get-tuple-element.35), channel_id=1, source_target_pairs={{0,8},{8,16},{16,24},{1,9},{9,17},{17,25},{2,10},{10,18},{18,26},{... | collective-permute-start | bytes 221192 | tf_op jit(solution)/shard_map/ppermute | solution.py:21
  123.5 10.4 %collective-permute-start.5 = (f32[144,1,128]{2,1,0:T(1,128)S(1)}, f32[144,1,128]{2,1,0:T(1,128)S(1)}, u32[]{:S(2)}, u32[]{:S(2)}) collective-permute-start(f32[144,1,128]{2,1,0:T(1,128)S(1)} %get-tuple-element.36), channel_id=1, source_target_pairs={{8,0},{16,8},{24,16},{9,1},{17,9},{25,17},{10,2},{18,10},{26,18},{... | collective-permute-start | bytes 221192 | tf_op jit(solution)/shard_map/ppermute | solution.py:23
  153.3 14.7 %copy-start = (f32[144,128,128]{2,1,0:T(8,128)S(1)}, f32[144,128,128]{2,1,0:T(8,128)}, u32[]{:S(2)}) copy-start(f32[144,128,128]{2,1,0:T(8,128)} %fusion.46) | copy-start | bytes 28311556
  168.0 14.1 %collective-permute-start.6 = (f32[144,1,128]{2,1,0:T(1,128)S(1)}, f32[144,1,128]{2,1,0:T(1,128)S(1)}, u32[]{:S(2)}, u32[]{:S(2)}) collective-permute-start(f32[144,1,128]{2,1,0:T(1,128)S(1)} %get-tuple-element.29), channel_id=1, source_target_pairs={{0,8},{8,16},{16,24},{1,9},{9,17},{17,25},{2,10},{10,18},{18,26},{... | collective-permute-start | bytes 221192 | tf_op jit(solution)/shard_map/ppermute | solution.py:21
  171.7 10.5 %collective-permute-start.7 = (f32[144,1,128]{2,1,0:T(1,128)S(1)}, f32[144,1,128]{2,1,0:T(1,128)S(1)}, u32[]{:S(2)}, u32[]{:S(2)}) collective-permute-start(f32[144,1,128]{2,1,0:T(1,128)S(1)} %get-tuple-element.30), channel_id=1, source_target_pairs={{8,0},{16,8},{24,16},{9,1},{17,9},{25,17},{10,2},{18,10},{26,18},{... | collective-permute-start | bytes 221192 | tf_op jit(solution)/shard_map/ppermute | solution.py:23
  201.5 14.7 %copy-start.1 = (f32[144,128,128]{2,1,0:T(8,128)S(1)}, f32[144,128,128]{2,1,0:T(8,128)}, u32[]{:S(2)}) copy-start(f32[144,128,128]{2,1,0:T(8,128)} %fusion.38) | copy-start | bytes 28311556
  216.3 14.3 %collective-permute-start.8 = (f32[144,1,128]{2,1,0:T(1,128)S(1)}, f32[144,1,128]{2,1,0:T(1,128)S(1)}, u32[]{:S(2)}, u32[]{:S(2)}) collective-permute-start(f32[144,1,128]{2,1,0:T(1,128)S(1)} %get-tuple-element.23), channel_id=1, source_target_pairs={{0,8},{8,16},{16,24},{1,9},{9,17},{17,25},{2,10},{10,18},{18,26},{... | collective-permute-start | bytes 221192 | tf_op jit(solution)/shard_map/ppermute | solution.py:21
  219.9 10.7 %collective-permute-start.9 = (f32[144,1,128]{2,1,0:T(1,128)S(1)}, f32[144,1,128]{2,1,0:T(1,128)S(1)}, u32[]{:S(2)}, u32[]{:S(2)}) collective-permute-start(f32[144,1,128]{2,1,0:T(1,128)S(1)} %get-tuple-element.24), channel_id=1, source_target_pairs={{8,0},{16,8},{24,16},{9,1},{17,9},{25,17},{10,2},{18,10},{26,18},{... | collective-permute-start | bytes 221192 | tf_op jit(solution)/shard_map/ppermute | solution.py:23
  250.0 14.7 %copy-start.2 = (f32[144,128,128]{2,1,0:T(8,128)S(1)}, f32[144,128,128]{2,1,0:T(8,128)}, u32[]{:S(2)}) copy-start(f32[144,128,128]{2,1,0:T(8,128)} %fusion.30) | copy-start | bytes 28311556
  264.7 14.0 %collective-permute-start.10 = (f32[144,1,128]{2,1,0:T(1,128)S(1)}, f32[144,1,128]{2,1,0:T(1,128)S(1)}, u32[]{:S(2)}, u32[]{:S(2)}) collective-permute-start(f32[144,1,128]{2,1,0:T(1,128)S(1)} %get-tuple-element.17), channel_id=1, source_target_pairs={{0,8},{8,16},{16,24},{1,9},{9,17},{17,25},{2,10},{10,18},{18,26},{... | collective-permute-start | bytes 221192 | tf_op jit(solution)/shard_map/ppermute | solution.py:21
  268.4 10.3 %collective-permute-start.11 = (f32[144,1,128]{2,1,0:T(1,128)S(1)}, f32[144,1,128]{2,1,0:T(1,128)S(1)}, u32[]{:S(2)}, u32[]{:S(2)}) collective-permute-start(f32[144,1,128]{2,1,0:T(1,128)S(1)} %get-tuple-element.18), channel_id=1, source_target_pairs={{8,0},{16,8},{24,16},{9,1},{17,9},{25,17},{10,2},{18,10},{26,18},{... | collective-permute-start | bytes 221192 | tf_op jit(solution)/shard_map/ppermute | solution.py:23
  297.9 11.1 %copy-start.8 = (f32[1152]{0:T(1024)S(1)}, f32[1152]{0:T(1024)}, u32[]{:S(2)}) copy-start(f32[1152]{0:T(1024)} %param.14) | copy-start | bytes 13828
  303.2 109.8 %all-to-all-start = ((bf16[144,128,128]{2,0,1:T(8,128)(2,1)}), bf16[144,128,128]{2,0,1:T(8,128)(2,1)}, u32[]{:S(2)}, u32[]{:S(2)}) async-start(bf16[144,128,128]{2,0,1:T(8,128)(2,1)} %copy.19), calls=%async_computation | async-start | bytes 9437184 | tf_op jit(solution)/shard_map/all_to_all | solution.py:90
  416.6 21.7 %copy-start.4 = (bf16[144,8,16,128]{3,2,0,1:T(8,128)(2,1)}, bf16[144,8,16,128]{3,2,0,1:T(8,128)(2,1)S(1)}, u32[]{:S(2)}) copy-start(bf16[144,8,16,128]{3,2,0,1:T(8,128)(2,1)S(1)} %copy.20) | copy-start | bytes 14155780
  416.6 9.9 %copy-start.10 = (bf16[1728,1152]{1,0:T(8,128)(2,1)S(1)}, bf16[1728,1152]{1,0:T(8,128)(2,1)}, u32[]{:S(2)}) copy-start(bf16[1728,1152]{1,0:T(8,128)(2,1)} %param.15) | copy-start | bytes 11943940
  482.0 110.1 %all-to-all-start.1 = ((bf16[1152,16,128]{2,1,0:T(8,128)(2,1)}), bf16[1152,16,128]{2,1,0:T(8,128)(2,1)}, u32[]{:S(2)}, u32[]{:S(2)}) async-start(bf16[1152,16,128]{2,1,0:T(8,128)(2,1)} %copy.22), calls=%async_computation.1 | async-start | bytes 9437184 | tf_op jit(solution)/shard_map/all_to_all | solution.py:91
  595.2 5.2 copy-start.5
  595.2 5.1 copy-start.6
  595.3 5.1 copy-start.9
  643.7 12.5 %collective-permute-start.12 = (f32[144,1,128]{2,1,0:T(1,128)S(1)}, f32[144,1,128]{2,1,0:T(1,128)S(1)}, u32[]{:S(2)}, u32[]{:S(2)}) collective-permute-start(f32[144,1,128]{2,1,0:T(1,128)S(1)} %get-tuple-element.11), channel_id=1, source_target_pairs={{0,8},{8,16},{16,24},{1,9},{9,17},{17,25},{2,10},{10,18},{18,26},{... | collective-permute-start | bytes 221192 | tf_op jit(solution)/shard_map/ppermute | solution.py:21
  645.7 10.5 %collective-permute-start.13 = (f32[144,1,128]{2,1,0:T(1,128)S(1)}, f32[144,1,128]{2,1,0:T(1,128)S(1)}, u32[]{:S(2)}, u32[]{:S(2)}) collective-permute-start(f32[144,1,128]{2,1,0:T(1,128)S(1)} %get-tuple-element.12), channel_id=1, source_target_pairs={{8,0},{16,8},{24,16},{9,1},{17,9},{25,17},{10,2},{18,10},{26,18},{... | collective-permute-start | bytes 221192 | tf_op jit(solution)/shard_map/ppermute | solution.py:23
where the time goes:
time: 683 us; the launch traced here: 675 us
  waiting for transfers between devices  209 us (31%)
  other arithmetic  196 us (29%)
  local copies, waits for them, and re-layouts  177 us (26%)
  starting transfers between devices  50.8 us (7%)
  matrix products  41.6 us (6%)
    slice x12, local copies, waits for them, and re-layouts, upwind(): eastern = jnp.roll(center, -1, axis=2)  120 us
    mul x5, other arithmetic, upwind(): return (center - change) * sea_mask  108 us
    all_to_all x1, waiting for transfers between devices, body(): lax.all_to_all(point_terms(gathered, dissipation, pair_first, pair_second...  105 us
    all_to_all x1, waiting for transfers between devices, body(): lax.all_to_all(outgoing, 'comp', split_axis=1, concat_axis=0, tiled=True)  104 us
    add x1, other arithmetic, body(): density = density + growth * density + returned.astype(jnp.float32)  34.9 us
    dot_general x1, matrix products, point_terms(): jnp.dot(merge_weight, product, preferred_element_type=jnp.float32)  29.8 us
    ppermute x7, starting transfers between devices, with_halo(): lax.ppermute(tail, axis, [(i, (i + 1) % count) for i in range(ends)])  24.6 us
    slice x2, local copies, waits for them, and re-layouts, upwind(): western = jnp.roll(center, 1, axis=2)  22.9 us
  transfers between devices with their start and end apart: 16, of which 2 were waited for; matrix products, arithmetic and copies ran while one was open for 12% of the time, Pallas kernels for 0%

commit v1 on v0

v1 whole, which is shorter than its diff:
```python
import functools
import math

import jax
import jax.numpy as jnp
from jax import lax
from jax.experimental import pallas as pl
from jax.experimental.pallas import tpu as pltpu
from jax.sharding import PartitionSpec as P

ND = 36
PROP_STEPS = 6
HALO = 8
SENDS = 3
RETURNS = 2
F32 = jnp.float32
BF16 = jnp.bfloat16
VMEM = pltpu.VMEM
SMEM = pltpu.SMEM


def edges(cells, axis_dim):
    count = lax.axis_size("geo")
    ends = count - 1
    size = cells.shape[axis_dim]
    head = lax.slice_in_dim(cells, 0, HALO, axis=axis_dim)
    tail = lax.slice_in_dim(cells, size - HALO, size, axis=axis_dim)
    lower = lax.ppermute(tail, "geo", [(i, i + 1) for i in range(ends)])
    upper = lax.ppermute(head, "geo", [(i + 1, i) for i in range(ends)])
    return lower, upper


def block_of(comps):
    return 16 if comps % 16 == 0 else comps


def stride_of(block):
    return -(-block // 8) * 8


def upwind(v, mask, coef, at):
    center, west, east, south, north = (coef[at + k] for k in range(5))
    rows = v.shape[0]
    moved = west * pltpu.roll(v, 1, 1) + east * pltpu.roll(v, v.shape[1] - 1, 1)
    moved = moved + south * pltpu.roll(v, 1, 0) + north * pltpu.roll(v, rows - 1, 0)
    return (center * v + moved) * mask


def prop_kernel(coef, lower, cells, upper, mask, density, outgoing, turned):
    block, rows, cols = cells.shape
    stride = stride_of(block)
    first = pl.program_id(0) * block

    def one(c, carry):
        v = jnp.concatenate(
            [lower[c].astype(F32), cells[c].astype(F32), upper[c].astype(F32)], axis=0
        )
        sea = mask[...]
        for _ in range(PROP_STEPS):
            v = upwind(v, sea, coef, (first + c) * 8)
        density[c] = v
        turned[pl.ds(c, rows, stride=stride), :] = v[HALO : HALO + rows]
        return carry

    lax.fori_loop(0, block, one, 0)

    def pack(r, carry):
        start = pl.multiple_of(r * stride, 8)
        outgoing[r] = turned[pl.ds(start, block), :].astype(BF16)
        return carry

    lax.fori_loop(0, rows, pack, 0, unroll=8)


def propagate(coef, lower, cells, upper, mask):
    comps, rows, cols = cells.shape
    block = block_of(comps)
    tall = rows + 2 * HALO
    return pl.pallas_call(
        prop_kernel,
        grid=(comps // block,),
        in_specs=[
            pl.BlockSpec(memory_space=SMEM),
            pl.BlockSpec((block, HALO, cols), lambda i: (i, 0, 0)),
            pl.BlockSpec((block, rows, cols), lambda i: (i, 0, 0)),
            pl.BlockSpec((block, HALO, cols), lambda i: (i, 0, 0)),
            pl.BlockSpec((tall, cols), lambda i: (0, 0)),
        ],
        out_specs=[
            pl.BlockSpec((block, tall, cols), lambda i: (i, 0, 0)),
            pl.BlockSpec((rows, block, cols), lambda i: (0, i, 0)),
        ],
        out_shape=[
            jax.ShapeDtypeStruct((comps, tall, cols), F32),
            jax.ShapeDtypeStruct((rows, comps, cols), BF16),
        ],
        scratch_shapes=[VMEM((rows * stride_of(block), cols), F32)],
        cost_estimate=pl.CostEstimate(
            flops=comps * tall * cols * 100,
            bytes_accessed=comps * tall * cols * 8,
            transcendentals=0,
        ),
        name="propagate",
    )(coef, lower, cells, upper, mask)


def point_kernel(sends, *refs):
    near, far = refs[:sends], refs[sends : 2 * sends]
    loss, first, second, merge, out, spectra, product = refs[2 * sends :]
    peers, _, part, cols = near[0].shape
    local = sends * part
    comps, terms = merge.shape
    for side, group in enumerate((near, far)):
        lanes = slice(side * cols, (side + 1) * cols)
        for k in range(sends):
            for s in range(peers):
                at = s * local + k * part
                spectra[at : at + part, lanes] = group[k][s, 0]
    tile = max(t for t in range(16, 600, 16) if terms % t == 0)

    def multiply(t, carry):
        rows = pl.ds(pl.multiple_of(t * tile, 16), tile)
        x = spectra[...]
        one = jnp.dot(first[rows, :], x, preferred_element_type=F32)
        two = jnp.dot(second[rows, :], x, preferred_element_type=F32)
        product[rows, :] = (one * two).astype(BF16)
        return carry

    lax.fori_loop(0, terms // tile, multiply, 0)
    energy = jnp.sum(spectra[...].astype(F32), axis=0, keepdims=True)
    root = jnp.sqrt(energy / comps + 1e-06)
    if peers == 1:
        step = max(t for t in range(16, 600, 16) if comps % t == 0)
        for d in range(0, comps, step):
            rows = slice(d, d + step)
            moved = jnp.dot(merge[rows, :], product[...], preferred_element_type=F32)
            total = moved - loss[rows, :] * root * spectra[rows, :].astype(F32)
            out[0, 0, rows] = total[:, :cols].astype(BF16)
            out[0, 1, rows] = total[:, cols:].astype(BF16)
        return
    share = max(g for g in range(1, peers + 1) if peers % g == 0 and g * local <= 600)
    for d in range(0, peers, share):
        rows = slice(d * local, (d + share) * local)
        moved = jnp.dot(merge[rows, :], product[...], preferred_element_type=F32)
        total = moved - loss[rows, :] * root * spectra[rows, :].astype(F32)
        for g in range(share):
            piece = total[g * local : (g + 1) * local].astype(BF16)
            out[d + g, 0] = piece[:, :cols]
            out[d + g, 1] = piece[:, cols:]


def point_terms(chunks, start, pairs, loss, first, second, merge):
    sends = len(chunks)
    peers, rows, part, cols = chunks[0].shape
    local = sends * part
    comps, terms = merge.shape
    whole = lambda shape: pl.BlockSpec(shape, lambda i: (0, 0))
    near = pl.BlockSpec((peers, 1, part, cols), lambda i: (0, start + i, 0, 0))
    far = pl.BlockSpec((peers, 1, part, cols), lambda i: (0, rows - 1 - start - i, 0, 0))
    return pl.pallas_call(
        functools.partial(point_kernel, sends),
        grid=(pairs,),
        in_specs=[near] * sends
        + [far] * sends
        + [whole((comps, 1)), whole((terms, comps)), whole((terms, comps)), whole((comps, terms))],
        out_specs=pl.BlockSpec((peers, 2, local, cols), lambda i: (0, i, 0, 0)),
        out_shape=jax.ShapeDtypeStruct((peers, 2 * pairs, local, cols), BF16),
        scratch_shapes=[VMEM((comps, 2 * cols), BF16), VMEM((terms, 2 * cols), BF16)],
        cost_estimate=pl.CostEstimate(
            flops=pairs * 12 * comps * terms * cols,
            bytes_accessed=6 * comps * terms + pairs * 8 * comps * cols,
            transcendentals=0,
        ),
        compiler_params=pltpu.CompilerParams(vmem_limit_bytes=60 * 1024 * 1024),
        name="points",
    )(*chunks, *chunks, loss, first, second, merge)


def final_kernel(returns, coef, density, low_inc, high_inc, wind, mask, *refs):
    incs = refs[:returns]
    out, turned = refs[returns:]
    block, rows, cols = out.shape
    peers, held = incs[0].shape[:2]
    band = rows // peers
    stride = stride_of(block)
    first = pl.program_id(0) * block

    def place(s, carry):
        for k in range(returns):
            for j in range(held):
                a = k * (held // 2) + j // 2
                row = a if j % 2 == 0 else band - 1 - a
                at = pl.multiple_of((s * band + row) * stride, 8)
                turned[pl.ds(at, block), :] = incs[k][s, j].astype(F32)
        return carry

    lax.fori_loop(0, peers, place, 0)

    def one(c, carry):
        at = (first + c) * 8
        inc = jnp.concatenate(
            [low_inc[c], turned[pl.ds(c, rows, stride=stride), :], high_inc[c]], axis=0
        )
        v = density[c]
        facing = jnp.maximum(coef[at + 6] * wind[1] + coef[at + 7] * wind[2], 0.0)
        growth = coef[at + 5] * wind[0] * facing * facing
        v = v + growth * v + inc
        v = upwind(v, mask[...], coef, at)
        out[c] = v[HALO : HALO + rows].astype(BF16)
        return carry

    lax.fori_loop(0, block, one, 0)


def finish(coef, density, low_inc, high_inc, wind, mask, incs, lead):
    local, tall, cols = density.shape
    rows = tall - 2 * HALO
    block = block_of(local)
    peers, held = incs[0].shape[:2]
    return pl.pallas_call(
        functools.partial(final_kernel, len(incs)),
        grid=(local // block,),
        in_specs=[
            pl.BlockSpec(memory_space=SMEM),
            pl.BlockSpec((block, tall, cols), lambda i: (i, 0, 0)),
            pl.BlockSpec((block, HALO, cols), lambda i: (i, 0, 0)),
            pl.BlockSpec((block, HALO, cols), lambda i: (i, 0, 0)),
            pl.BlockSpec((3, tall, cols), lambda i: (0, 0, 0)),
            pl.BlockSpec((tall, cols), lambda i: (0, 0)),
        ]
        + [pl.BlockSpec((peers, held, block, cols), lambda i: (0, 0, i, 0))] * len(incs),
        out_specs=pl.BlockSpec((block, rows, cols), lambda i: (i, 0, 0)),
        out_shape=jax.ShapeDtypeStruct((local, rows, cols), BF16),
        scratch_shapes=[VMEM((rows * stride_of(block), cols), F32)],
        name="finish",
    )(coef, density, low_inc, high_inc, wind, mask, *incs)


def body(spectrum, land_mask, wind_speed, wind_dir, input_rate, dissipation, pair_first, pair_second, merge_weight):
    local, rows, cols = spectrum.shape
    peers = lax.axis_size("comp")
    band = rows // peers
    ids = lax.axis_index("comp") * local + jnp.arange(local, dtype=jnp.int32)
    frequency = (ids // ND).astype(F32)
    heading = 2.0 * math.pi * (ids % ND).astype(F32) / ND
    courant = 0.7 * jnp.power(F32(1.1), -frequency)
    cos_h, sin_h = jnp.cos(heading), jnp.sin(heading)
    west, east = jnp.maximum(courant * cos_h, 0.0), jnp.maximum(-courant * cos_h, 0.0)
    south, north = jnp.maximum(courant * sin_h, 0.0), jnp.maximum(-courant * sin_h, 0.0)
    center = 1.0 - west - east - south - north
    coef = jnp.stack([center, west, east, south, north, input_rate, cos_h, sin_h], axis=1).reshape(-1)

    lower, upper = edges(spectrum, 1)
    fields = jnp.stack([wind_speed, jnp.cos(wind_dir), jnp.sin(wind_dir), land_mask.astype(F32)])
    low_f, high_f = edges(fields, 1)
    fields = jnp.concatenate([low_f, fields, high_f], axis=1)
    wind, mask = fields[:3], fields[3]

    whole_tiles = local % (16 * SENDS) == 0
    sends = SENDS if whole_tiles else 1
    part = local // sends
    density, chunks = [], []
    for k in range(sends):
        cut = slice(k * part, (k + 1) * part)
        d, out = propagate(coef[k * part * 8 : (k + 1) * part * 8], lower[cut], spectrum[cut], upper[cut], mask)
        density.append(d)
        out = out.reshape(peers, band, part, cols)
        chunks.append(lax.all_to_all(out, "comp", split_axis=0, concat_axis=0, tiled=True))
    density = jnp.concatenate(density, axis=0)

    loss = dissipation[:, None]
    if not whole_tiles:
        chunks = [c.transpose(1, 0, 2, 3).reshape(1, band, peers * local, cols) for c in chunks]
    returns = max(1, min(RETURNS, band // 2))
    pairs = band // 2 // returns
    incs = []
    for k in range(returns):
        inc = point_terms(chunks, k * pairs, pairs, loss, pair_first, pair_second, merge_weight)
        if not whole_tiles:
            inc = inc.reshape(2 * pairs, peers, local, cols).transpose(1, 0, 2, 3)
        incs.append(lax.all_to_all(inc, "comp", split_axis=0, concat_axis=0, tiled=True))
    count = lax.axis_size("geo")
    ends = count - 1
    low = lax.ppermute(incs[0][peers - 1, 1], "geo", [(i, i + 1) for i in range(ends)])
    high = lax.ppermute(incs[0][0, 0], "geo", [(i + 1, i) for i in range(ends)])
    low = jnp.pad(low.astype(F32)[:, None], ((0, 0), (HALO - 1, 0), (0, 0)))
    high = jnp.pad(high.astype(F32)[:, None], ((0, 0), (0, HALO - 1), (0, 0)))
    return finish(coef, density, low, high, wind, mask, incs, HALO)


def solution(mesh):
    placed = (P("comp", "geo", None), P("geo", None), P("geo", None), P("geo", None), P("comp"), P(), P(), P(), P())
    return jax.shard_map(
        body, mesh=mesh, in_specs=placed, out_specs=P("comp", "geo", None), check_vma=False
    )
```

time: 683 us -> 345 us (0.51)
  other arithmetic: 196 us -> 12.3 us
  Pallas kernels: 0 us -> 165 us
  local copies, waits for them, and re-layouts: 177 us -> 21 us
  waiting for transfers between devices: 209 us -> 103 us
  matrix products: 41.6 us -> 0 us
  starting transfers between devices: 50.8 us -> 39.6 us
    pallas_call x0 -> x6, Pallas kernels: none -> 165 us  [the longest x3 95.2 us: propagate(): pl.pallas_call(prop_kernel, grid=(comps // block,), in_specs=[pl.BlockSpe...]
    slice x21 -> x11, local copies, waits for them, and re-layouts: 144 us -> 9.69 us  [the longest x1 4.75 us: body(): spectrum[cut]]
    all_to_all x2 -> x5, waiting for transfers between devices: 209 us -> 101 us  [the longest x2 63.2 us: body(): lax.all_to_all(inc, 'comp', split_axis=0, concat_axis=0, tiled=True)]
    mul x5 -> x0, other arithmetic: 108 us -> none  [upwind(): return (center - change) * sea_mask]
    convert_element_type x5 -> x0, other arithmetic: 47.6 us -> none  [the longest x1 19.2 us: body(): outgoing = density.astype(jnp.bfloat16)]
    dot_general x2 -> x0, matrix products: 41.6 us -> none  [the longest x1 29.8 us: point_terms(): jnp.dot(merge_weight, product, preferred_element_type=jnp.float32)]
    add x1 -> x0, other arithmetic: 34.9 us -> none  [body(): density = density + growth * density + returned.astype(jnp.float32)]
    ppermute x14 -> x6, starting transfers between devices: 40 us -> 16.7 us  [the longest x2 8.14 us: edges(): lower = lax.ppermute(tail, 'geo', [(i, i + 1) for i in range(ends)])]
  transfers between devices with their start and end apart: 16 -> 11, of which waited for: 2 -> 6; matrix products, arithmetic and copies ran while one was open for 12% -> 9% of each run, Pallas kernels for 0% -> 25%
where the time goes in v1:
time: 345 us; the launch traced here: 341 us
  Pallas kernels  165 us (48%)
  waiting for transfers between devices  103 us (30%)
  starting transfers between devices  39.6 us (11%)
  local copies, waits for them, and re-layouts  21 us (6%)
  other arithmetic  12.3 us (4%)
    pallas_call x3, Pallas kernels, propagate(): pl.pallas_call(prop_kernel, grid=(comps // block,), in_specs=[pl.BlockSpe...  95.2 us
    all_to_all x2, waiting for transfers between devices, body(): lax.all_to_all(inc, 'comp', split_axis=0, concat_axis=0, tiled=True)  63.2 us
    pallas_call x2, Pallas kernels, point_terms(): pl.pallas_call(functools.partial(point_kernel, sends), grid=(pairs,), in_...  45.4 us
    all_to_all x3, waiting for transfers between devices, body(): lax.all_to_all(out, 'comp', split_axis=0, concat_axis=0, tiled=True)  37.4 us
    pallas_call x1, Pallas kernels, finish(): pl.pallas_call(functools.partial(final_kernel, len(incs)), grid=(local //...  24.6 us
    all_to_all x3, starting transfers between devices, body(): lax.all_to_all(out, 'comp', split_axis=0, concat_axis=0, tiled=True)  13.6 us
    all_to_all x2, starting transfers between devices, body(): lax.all_to_all(inc, 'comp', split_axis=0, concat_axis=0, tiled=True)  9.34 us
    concatenate x1, other arithmetic, body(): density = jnp.concatenate(density, axis=0)  9.02 us
  transfers between devices with their start and end apart: 11, of which 6 were waited for; matrix products, arithmetic and copies ran while one was open for 9% of the time, Pallas kernels for 25%

profile of v1, /device:TPU:1, one launch (start us, length us, event | category | flops | bytes accessed | tf_op | source)
XLA Modules:
  0.0 341.5 jit_solution(4999712243572808370)
XLA Ops:
  0.0 1.1 fusion.6
  1.1 4.5 %collective-permute-start = (bf16[144,8,128]{2,1,0:T(8,128)(2,1)S(1)}, bf16[144,8,128]{2,1,0:T(8,128)(2,1)S(1)}, u32[]{:S(2)}, u32[]{:S(2)}) collective-permute-start(bf16[144,8,128]{2,1,0:T(8,128)(2,1)S(1)} %get-tuple-element.21), channel_id=1, source_target_pairs={{0,8},{8,16},{16,24},{1,9},{9,17},{17,25},{2,10},{10,18},{18,26},{... | collective-permute-start | bytes 884744 | tf_op jit(solution)/shard_map/ppermute | solution.py:28
  5.6 1.9 collective-permute-start.1
  7.5 0.8 convert_bitcast_fusion
  8.4 1.1 cosine_bitcast_fusion
  10.2 1.9 collective-permute-start.3
  12.1 3.6 %collective-permute-start.2 = (f32[4,8,128]{2,1,0:T(8,128)S(1)}, f32[4,8,128]{2,1,0:T(8,128)S(1)}, u32[]{:S(2)}, u32[]{:S(2)}) collective-permute-start(f32[4,8,128]{2,1,0:T(8,128)S(1)} %get-tuple-element.30), channel_id=1, source_target_pairs={{0,8},{8,16},{16,24},{1,9},{9,17},{17,25},{2,10},{10,18},{18,26},{... | collective-permute-start | bytes 49160 | tf_op jit(solution)/shard_map/ppermute | solution.py:28
  16.1 4.8 %fusion.5 = (bf16[48,128,128]{2,1,0:T(8,128)(2,1)}, bf16[48,128,128]{2,1,0:T(8,128)(2,1)}, bf16[48,128,128]{2,1,0:T(8,128)(2,1)}) fusion(bf16[144,128,128]{2,1,0:T(8,128)(2,1)} %param.9), kind=kLoop, calls=%fused_computation.32 | loop fusion | bytes 9437184 | tf_op jit(solution)/shard_map/slice | solution.py:265
  23.8 31.8 %propagate.3 = (f32[48,144,128]{2,1,0:T(8,128)}, bf16[128,48,128]{2,1,0:T(8,128)(2,1)}) custom-call(f32[384]{0:T(512)} %slice.70.coef, bf16[48,8,128]{2,1,0:T(8,128)(2,1)} %get-tuple-element.27.lower, bf16[48,128,128]{2,1,0:T(8,128)(2,1)} %get-tuple-element.17.cells, bf16[48,8,128]{2,1,0:T(8,128)(2,1)} %get-tuple-element.24.upper, ...), custom_call_target="tpu_custom_call" | custom-call | flops 88473600 | bytes 7077888 | tf_op jit(solution)/shard_map/propagate/pallas_call | solution.py:79
  55.6 5.6 %all-to-all-start = ((bf16[8,16,48,128]{3,2,1,0:T(8,128)(2,1)}), bf16[8,16,48,128]{3,2,1,0:T(8,128)(2,1)S(1)}, u32[]{:S(2)}, u32[]{:S(2)}) async-start(bf16[8,16,48,128]{3,2,1,0:T(8,128)(2,1)} %bitcast.20), calls=%async_computation | async-start | bytes 3145728 | tf_op jit(solution)/shard_map/all_to_all | solution.py:268
  61.9 31.7 %propagate.4 = (f32[48,144,128]{2,1,0:T(8,128)}, bf16[128,48,128]{2,1,0:T(8,128)(2,1)}) custom-call(f32[384]{0:T(512)} %slice.80.coef, bf16[48,8,128]{2,1,0:T(8,128)(2,1)} %get-tuple-element.29.lower, bf16[48,128,128]{2,1,0:T(8,128)(2,1)} %get-tuple-element.19.cells, bf16[48,8,128]{2,1,0:T(8,128)(2,1)} %get-tuple-element.26.upper, ...), custom_call_target="tpu_custom_call" | custom-call | flops 88473600 | bytes 7077888 | tf_op jit(solution)/shard_map/propagate/pallas_call | solution.py:79
  93.6 4.7 %all-to-all-done.refs_0_.refs_3_ = bf16[8,16,48,128]{3,2,1,0:T(8,128)(2,1)S(1)} async-done(((bf16[8,16,48,128]{3,2,1,0:T(8,128)(2,1)}), bf16[8,16,48,128]{3,2,1,0:T(8,128)(2,1)S(1)}, u32[]{:S(2)}, u32[]{:S(2)}) %all-to-all-start) | async-done | bytes 1572896 | tf_op jit(solution)/shard_map/all_to_all | solution.py:268
  98.3 3.7 %all-to-all-start.1 = ((bf16[8,16,48,128]{3,2,1,0:T(8,128)(2,1)}), bf16[8,16,48,128]{3,2,1,0:T(8,128)(2,1)S(1)}, u32[]{:S(2)}, u32[]{:S(2)}) async-start(bf16[8,16,48,128]{3,2,1,0:T(8,128)(2,1)} %bitcast.19), calls=%async_computation.1 | async-start | bytes 3145728 | tf_op jit(solution)/shard_map/all_to_all | solution.py:268
  102.8 31.7 %propagate.5 = (f32[48,144,128]{2,1,0:T(8,128)}, bf16[128,48,128]{2,1,0:T(8,128)(2,1)}) custom-call(f32[384]{0:T(512)} %slice.85.coef, bf16[48,8,128]{2,1,0:T(8,128)(2,1)} %get-tuple-element.28.lower, bf16[48,128,128]{2,1,0:T(8,128)(2,1)} %get-tuple-element.18.cells, bf16[48,8,128]{2,1,0:T(8,128)(2,1)} %get-tuple-element.25.upper, ...), custom_call_target="tpu_custom_call" | custom-call | flops 88473600 | bytes 7077888 | tf_op jit(solution)/shard_map/propagate/pallas_call | solution.py:79
  134.5 4.1 %all-to-all-done.1.refs_1_.refs_4_ = bf16[8,16,48,128]{3,2,1,0:T(8,128)(2,1)S(1)} async-done(((bf16[8,16,48,128]{3,2,1,0:T(8,128)(2,1)}), bf16[8,16,48,128]{3,2,1,0:T(8,128)(2,1)S(1)}, u32[]{:S(2)}, u32[]{:S(2)}) %all-to-all-start.1) | async-done | bytes 1572896 | tf_op jit(solution)/shard_map/all_to_all | solution.py:268
  138.7 4.3 %all-to-all-start.2 = ((bf16[8,16,48,128]{3,2,1,0:T(8,128)(2,1)}), bf16[8,16,48,128]{3,2,1,0:T(8,128)(2,1)}, u32[]{:S(2)}, u32[]{:S(2)}) async-start(bf16[8,16,48,128]{3,2,1,0:T(8,128)(2,1)} %bitcast.21), calls=%async_computation.2 | async-start | bytes 3145728 | tf_op jit(solution)/shard_map/all_to_all | solution.py:268
  143.0 1.1 broadcast_in_dim.14.refs_6_
  144.1 6.3 %copy.19.refs_9_ = bf16[1152,1728]{1,0:T(8,128)(2,1)} copy(bf16[1152,1728]{0,1:T(8,128)(2,1)} %param.17) | data formatting | bytes 7962624 | tf_op args[8]
  150.4 28.5 %all-to-all-done.2.refs_2_.refs_5_ = bf16[8,16,48,128]{3,2,1,0:T(8,128)(2,1)} async-done(((bf16[8,16,48,128]{3,2,1,0:T(8,128)(2,1)}), bf16[8,16,48,128]{3,2,1,0:T(8,128)(2,1)}, u32[]{:S(2)}, u32[]{:S(2)}) %all-to-all-start.2) | async-done | bytes 1572896 | tf_op jit(solution)/shard_map/all_to_all | solution.py:268
  178.9 22.7 %points.2 = bf16[8,8,144,128]{3,2,1,0:T(8,128)(2,1)} custom-call(bf16[8,16,48,128]{3,2,1,0:T(8,128)(2,1)} %copy-done.1, bf16[8,16,48,128]{3,2,1,0:T(8,128)(2,1)} %copy-done.2, bf16[8,16,48,128]{3,2,1,0:T(8,128)(2,1)} %all-to-all-done.2.refs_2_.refs_5_, bf16[8,16,48,128]{3,2,1,0:T(8,128)(2,1)} %copy-done.1, bf16[8,16,48,128]{3,2,1,0:T(8,128)(2,1)} %copy-done.2, ...), custom_call_target="tpu_custom_call" | custom-call | flops 12230590464 | bytes 16662528 | tf_op jit(solution)/shard_map/points/pallas_call | solution.py:160
  201.6 4.9 %all-to-all-start.3 = ((bf16[8,8,144,128]{3,2,1,0:T(8,128)(2,1)}), bf16[8,8,144,128]{3,2,1,0:T(8,128)(2,1)S(1)}, u32[]{:S(2)}, u32[]{:S(2)}) async-start(bf16[8,8,144,128]{3,2,1,0:T(8,128)(2,1)} %points.2), calls=%async_computation.3 | async-start | bytes 4718592 | tf_op jit(solution)/shard_map/all_to_all | solution.py:281
  206.4 22.7 %points.3 = bf16[8,8,144,128]{3,2,1,0:T(8,128)(2,1)} custom-call(bf16[8,16,48,128]{3,2,1,0:T(8,128)(2,1)} %copy-done.1, bf16[8,16,48,128]{3,2,1,0:T(8,128)(2,1)} %copy-done.2, bf16[8,16,48,128]{3,2,1,0:T(8,128)(2,1)} %all-to-all-done.2.refs_2_.refs_5_, bf16[8,16,48,128]{3,2,1,0:T(8,128)(2,1)} %copy-done.1, bf16[8,16,48,128]{3,2,1,0:T(8,128)(2,1)} %copy-done.2, ...), custom_call_target="tpu_custom_call" | custom-call | flops 12230590464 | bytes 16662528 | tf_op jit(solution)/shard_map/points/pallas_call | solution.py:160
  229.1 30.5 %all-to-all-done.3.refs_0_ = bf16[8,8,144,128]{3,2,1,0:T(8,128)(2,1)S(1)} async-done(((bf16[8,8,144,128]{3,2,1,0:T(8,128)(2,1)}), bf16[8,8,144,128]{3,2,1,0:T(8,128)(2,1)S(1)}, u32[]{:S(2)}, u32[]{:S(2)}) %all-to-all-start.3) | async-done | bytes 2359328 | tf_op jit(solution)/shard_map/all_to_all | solution.py:281
  259.7 4.4 %all-to-all-start.4 = ((bf16[8,8,144,128]{3,2,1,0:T(8,128)(2,1)}), bf16[8,8,144,128]{3,2,1,0:T(8,128)(2,1)}, u32[]{:S(2)}, u32[]{:S(2)}) async-start(bf16[8,8,144,128]{3,2,1,0:T(8,128)(2,1)} %points.3), calls=%async_computation.4 | async-start | bytes 4718592 | tf_op jit(solution)/shard_map/all_to_all | solution.py:281
  265.6 2.8 collective-permute-start.4
  268.5 9.0 %pad_maximum_fusion.density = f32[144,144,128]{2,1,0:T(8,128)} fusion(f32[48,144,128]{2,1,0:T(8,128)} %get-tuple-element.13, f32[48,144,128]{2,1,0:T(8,128)} %get-tuple-element.12, f32[48,144,128]{2,1,0:T(8,128)} %get-tuple-element.11), kind=kLoop, calls=%fused_computation | loop fusion | flops 5308416 | bytes 21233664 | tf_op jit(solution)/shard_map/concatenate | solution.py:269
  277.5 1.9 collective-permute-start.5
  279.5 1.0 copy.22.low_inc
  280.5 2.7 collective-permute-done.5
  283.2 1.0 copy.23.high_inc
  284.2 32.6 %all-to-all-done.4.refs_1_ = bf16[8,8,144,128]{3,2,1,0:T(8,128)(2,1)} async-done(((bf16[8,8,144,128]{3,2,1,0:T(8,128)(2,1)}), bf16[8,8,144,128]{3,2,1,0:T(8,128)(2,1)}, u32[]{:S(2)}, u32[]{:S(2)}) %all-to-all-start.4) | async-done | bytes 2359328 | tf_op jit(solution)/shard_map/all_to_all | solution.py:281
  316.8 24.6 %finish.1 = bf16[144,128,128]{2,1,0:T(8,128)(2,1)} custom-call(f32[1152]{0:T(1024)} %reshape.127.coef, f32[144,144,128]{2,1,0:T(8,128)} %pad_maximum_fusion.density, f32[144,8,128]{2,1,0:T(8,128)} %copy.22.low_inc, f32[144,8,128]{2,1,0:T(8,128)} %copy.23.high_inc, f32[3,144,128]{2,1,0:T(8,128)} %pad_maximum_fusion.1.wind, ...), custom_call_target="tpu_custom_call" | custom-call | tf_op jit(solution)/shard_map/finish/pallas_call | solution.py:220
  (39 shorter events, 7.1 us)
Async XLA Ops:
  1.1 21.2 %collective-permute-start = (bf16[144,8,128]{2,1,0:T(8,128)(2,1)S(1)}, bf16[144,8,128]{2,1,0:T(8,128)(2,1)S(1)}, u32[]{:S(2)}, u32[]{:S(2)}) collective-permute-start(bf16[144,8,128]{2,1,0:T(8,128)(2,1)S(1)} %get-tuple-element.21), channel_id=1, source_target_pairs={{0,8},{8,16},{16,24},{1,9},{9,17},{17,25},{2,10},{10,18},{18,26},{... | collective-permute-start | bytes 884744 | tf_op jit(solution)/shard_map/ppermute | solution.py:28
  5.6 17.5 %collective-permute-start.1 = (bf16[144,8,128]{2,1,0:T(8,128)(2,1)S(1)}, bf16[144,8,128]{2,1,0:T(8,128)(2,1)S(1)}, u32[]{:S(2)}, u32[]{:S(2)}) collective-permute-start(bf16[144,8,128]{2,1,0:T(8,128)(2,1)S(1)} %get-tuple-element.20), channel_id=1, source_target_pairs={{8,0},{16,8},{24,16},{9,1},{17,9},{25,17},{10,2},{18,10},{26,18},{... | collective-permute-start | bytes 884744 | tf_op jit(solution)/shard_map/ppermute | solution.py:29
  10.2 11.5 %collective-permute-start.3 = (f32[4,8,128]{2,1,0:T(8,128)S(1)}, f32[4,8,128]{2,1,0:T(8,128)S(1)}, u32[]{:S(2)}, u32[]{:S(2)}) collective-permute-start(f32[4,8,128]{2,1,0:T(8,128)S(1)} %get-tuple-element.31), channel_id=1, source_target_pairs={{8,0},{16,8},{24,16},{9,1},{17,9},{25,17},{10,2},{18,10},{26,18},{... | collective-permute-start | bytes 49160 | tf_op jit(solution)/shard_map/ppermute | solution.py:29
  12.1 9.6 %collective-permute-start.2 = (f32[4,8,128]{2,1,0:T(8,128)S(1)}, f32[4,8,128]{2,1,0:T(8,128)S(1)}, u32[]{:S(2)}, u32[]{:S(2)}) collective-permute-start(f32[4,8,128]{2,1,0:T(8,128)S(1)} %get-tuple-element.30), channel_id=1, source_target_pairs={{0,8},{8,16},{16,24},{1,9},{9,17},{17,25},{2,10},{10,18},{18,26},{... | collective-permute-start | bytes 49160 | tf_op jit(solution)/shard_map/ppermute | solution.py:28
  16.0 4.8 %copy-start.5 = (f32[144]{0:T(256)S(1)}, f32[144]{0:T(256)}, u32[]{:S(2)}) copy-start(f32[144]{0:T(256)} %param.13) | copy-start | bytes 1732
  16.0 5.6 %copy-start.3 = (f32[128,128]{1,0:T(8,128)S(1)}, f32[128,128]{1,0:T(8,128)}, u32[]{:S(2)}) copy-start(f32[128,128]{1,0:T(8,128)} %param.11) | copy-start | bytes 196612
  55.6 42.7 %all-to-all-start = ((bf16[8,16,48,128]{3,2,1,0:T(8,128)(2,1)}), bf16[8,16,48,128]{3,2,1,0:T(8,128)(2,1)S(1)}, u32[]{:S(2)}, u32[]{:S(2)}) async-start(bf16[8,16,48,128]{3,2,1,0:T(8,128)(2,1)} %bitcast.20), calls=%async_computation | async-start | bytes 3145728 | tf_op jit(solution)/shard_map/all_to_all | solution.py:268
  98.3 40.4 %copy-start.1 = (bf16[8,16,48,128]{3,2,1,0:T(8,128)(2,1)}, bf16[8,16,48,128]{3,2,1,0:T(8,128)(2,1)S(1)}, u32[]{:S(2)}) copy-start(bf16[8,16,48,128]{3,2,1,0:T(8,128)(2,1)S(1)} %all-to-all-done.refs_0_.refs_3_) | copy-start | bytes 4718596
  98.3 44.7 %copy-start.4 = (f32[1152]{0:T(1024)S(1)}, f32[1152]{0:T(1024)}, u32[]{:S(2)}) copy-start(f32[1152]{0:T(1024)} %param.14) | copy-start | bytes 13828
  98.3 40.4 %all-to-all-start.1 = ((bf16[8,16,48,128]{3,2,1,0:T(8,128)(2,1)}), bf16[8,16,48,128]{3,2,1,0:T(8,128)(2,1)S(1)}, u32[]{:S(2)}, u32[]{:S(2)}) async-start(bf16[8,16,48,128]{3,2,1,0:T(8,128)(2,1)} %bitcast.19), calls=%async_computation.1 | async-start | bytes 3145728 | tf_op jit(solution)/shard_map/all_to_all | solution.py:268
  138.7 11.7 %copy-start.2 = (bf16[8,16,48,128]{3,2,1,0:T(8,128)(2,1)}, bf16[8,16,48,128]{3,2,1,0:T(8,128)(2,1)S(1)}, u32[]{:S(2)}) copy-start(bf16[8,16,48,128]{3,2,1,0:T(8,128)(2,1)S(1)} %all-to-all-done.1.refs_1_.refs_4_) | copy-start | bytes 4718596
  138.7 40.2 %all-to-all-start.2 = ((bf16[8,16,48,128]{3,2,1,0:T(8,128)(2,1)}), bf16[8,16,48,128]{3,2,1,0:T(8,128)(2,1)}, u32[]{:S(2)}, u32[]{:S(2)}) async-start(bf16[8,16,48,128]{3,2,1,0:T(8,128)(2,1)} %bitcast.21), calls=%async_computation.2 | async-start | bytes 3145728 | tf_op jit(solution)/shard_map/all_to_all | solution.py:268
  201.6 58.1 %all-to-all-start.3 = ((bf16[8,8,144,128]{3,2,1,0:T(8,128)(2,1)}), bf16[8,8,144,128]{3,2,1,0:T(8,128)(2,1)S(1)}, u32[]{:S(2)}, u32[]{:S(2)}) async-start(bf16[8,8,144,128]{3,2,1,0:T(8,128)(2,1)} %points.2), calls=%async_computation.3 | async-start | bytes 4718592 | tf_op jit(solution)/shard_map/all_to_all | solution.py:281
  259.7 17.8 %copy-start = (bf16[8,8,144,128]{3,2,1,0:T(8,128)(2,1)}, bf16[8,8,144,128]{3,2,1,0:T(8,128)(2,1)S(1)}, u32[]{:S(2)}) copy-start(bf16[8,8,144,128]{3,2,1,0:T(8,128)(2,1)S(1)} %all-to-all-done.3.refs_0_) | copy-start | bytes 7077892
  259.7 57.2 %all-to-all-start.4 = ((bf16[8,8,144,128]{3,2,1,0:T(8,128)(2,1)}), bf16[8,8,144,128]{3,2,1,0:T(8,128)(2,1)}, u32[]{:S(2)}, u32[]{:S(2)}) async-start(bf16[8,8,144,128]{3,2,1,0:T(8,128)(2,1)} %points.3), calls=%async_computation.4 | async-start | bytes 4718592 | tf_op jit(solution)/shard_map/all_to_all | solution.py:281
  265.6 13.8 %collective-permute-start.4 = (bf16[144,128]{1,0:T(8,128)(2,1)S(1)}, bf16[144,128]{1,0:T(8,128)(2,1)S(1)}, u32[]{:S(2)}, u32[]{:S(2)}) collective-permute-start(bf16[144,128]{1,0:T(8,128)(2,1)S(1)} %get-tuple-element.23), channel_id=1, source_target_pairs={{0,8},{8,16},{16,24},{1,9},{9,17},{17,25},{2,10},{10,18},{18,26},{... | collective-permute-start | bytes 110600 | tf_op jit(solution)/shard_map/ppermute | solution.py:284
  277.5 5.7 %collective-permute-start.5 = (bf16[144,128]{1,0:T(8,128)(2,1)S(1)}, bf16[144,128]{1,0:T(8,128)(2,1)S(1)}, u32[]{:S(2)}, u32[]{:S(2)}) collective-permute-start(bf16[144,128]{1,0:T(8,128)(2,1)S(1)} %get-tuple-element.22), channel_id=1, source_target_pairs={{8,0},{16,8},{24,16},{9,1},{17,9},{25,17},{10,2},{18,10},{26,18},{... | collective-permute-start | bytes 110600 | tf_op jit(solution)/shard_map/ppermute | solution.py:285
